TPU v7x, 32 devices: a whole 2x2x4 slice. The times are simulated.
32 devices in a mesh: gx: 4 (over z), gy: 8 (over y, x, core).
Axes of the slice: x: 2, y: 2, z: 4, core: 2. Of those that a mesh axis runs over, the one named last changes fastest.
Arguments:
- matrix_rows: float32 [4096, 1024], P(('gx', 'gy')), may hold values from -1.1 to 1.1
- tile_owner: int32 [136], replicated, may hold values from 0 to 31, as said below
- tile_slot: int32 [136], replicated, may hold values from 0 to 4, as said below
Outputs:
- packed_tiles: float32 [160, 256, 256], P(('gx', 'gy'))
Inputs may be any that keep to these rules, and one draw needn't show every extreme that they name: `tile_owner`: give tile (I, J) the class (c, r) as follows, with a = I // 4, b = J // 4, i = I % 4, j = J % 4: if a == b, c = a and r = i when i - j < 2, else r = j; if a > b and (a - b > 2, or a - b == 2 with i + j even), c = b and r = i; otherwise c = a and r = j. The owner of a class (c, r) tile is one of the devices c * 8 to c * 8 + 7. Every owner holds 4 or 5 tiles. At most 2 tiles of one class share an owner, and in every draw some owner holds exactly 2 tiles of one class. `tile_slot`: the tiles of one owner take the slots 0 to their count - 1, each once.
All inputs are finite; a program needn't handle non-finite values.
Results may differ from a plain program's by a relative error of at most 0.0003.
Values sent between devices are 32-bit elements; how exact they have to be, the bound alone decides.
A program may use at most 128 MiB of HBM per device.

v0:
```python
import jax
import jax.numpy as jnp
import numpy as np
from jax import lax
from jax.sharding import PartitionSpec as P


def from_behind(value, axis, steps):
    count = lax.axis_size(axis)
    pairs = [(source, (source + steps) % count) for source in range(count)]
    return lax.ppermute(value, axis, pairs)


def classify(row_tile, col_tile, half_tiles, count_x):
    group_a = row_tile // half_tiles
    group_b = col_tile // half_tiles
    inner_i = row_tile % half_tiles
    inner_j = col_tile % half_tiles
    same = group_a == group_b
    within_row = inner_i - inner_j < half_tiles // 2
    gap = group_a - group_b
    across_row = jnp.logical_or(
        gap > count_x // 2, jnp.logical_and(gap == count_x // 2, (inner_i + inner_j) % 2 == 0)
    )
    rowwise = jnp.where(same, within_row, across_row)
    class_r = jnp.where(rowwise, inner_i, inner_j)
    return (class_r, rowwise)


def per_device(matrix_rows, tile_owner, tile_slot):
    rows_dev, width = matrix_rows.shape
    tile_size = 2 * rows_dev
    count_x = lax.axis_size("gx")
    count_y = lax.axis_size("gy")
    half_tiles = count_y // 2
    half_x = count_x // 2
    capacity = count_x // 4 + 1
    devices = count_x * count_y
    tile_count = devices // 2
    lower_count = tile_owner.shape[0]
    slot_count = (lower_count + devices - 1) // devices
    x_index = lax.axis_index("gx")
    y_index = lax.axis_index("gy")
    own_r = y_index // 2
    own_h = y_index % 2
    shifted = [matrix_rows]
    for step in range(1, half_x + 1):
        shifted.append(from_behind(matrix_rows, "gx", step))
    first_count = half_tiles // 2 + 1
    offsets = jnp.arange(first_count, dtype=jnp.int32)
    first_cols = (own_r - offsets) % half_tiles
    first_valid = jnp.logical_or(offsets < half_tiles // 2, own_r < half_tiles // 2)
    flag = (x_index >= half_x).astype(jnp.int32)
    last_cols = 2 * jnp.arange(half_tiles // 2, dtype=jnp.int32) + (own_r + flag) % 2
    middle = half_x - 1
    middle_cols = jnp.tile(jnp.arange(half_tiles, dtype=jnp.int32), middle)
    col_of = jnp.concatenate([first_cols, middle_cols, last_cols])
    valid = jnp.concatenate([first_valid, jnp.ones((middle * half_tiles + half_tiles // 2,), bool)])
    step_table = np.concatenate(
        [
            np.zeros(first_count, np.int32),
            np.repeat(np.arange(1, half_x, dtype=np.int32), half_tiles),
            np.full(half_tiles // 2, half_x, np.int32),
        ]
    )
    step_of = jnp.asarray(step_table, jnp.int32)
    stacked = jnp.stack(shifted)
    full = jnp.einsum(
        "srk,ck->src",
        stacked,
        lax.all_gather(matrix_rows, "gy", axis=0, tiled=True),
        precision=lax.Precision.HIGHEST,
        preferred_element_type=jnp.float32,
    )
    full = full.reshape(half_x + 1, rows_dev, half_tiles, tile_size)
    pieces = full[step_of, :, col_of, :]
    source_x = (x_index - step_of) % count_x
    rowwise = jnp.where(step_of == 0, col_of <= own_r, source_x > x_index)
    row_tile = jnp.where(rowwise, source_x * half_tiles + own_r, x_index * half_tiles + col_of)
    col_tile = jnp.where(rowwise, x_index * half_tiles + col_of, source_x * half_tiles + own_r)
    row_inside = own_h * rows_dev + lax.broadcasted_iota(jnp.int32, (rows_dev, tile_size), 0)
    col_inside = lax.broadcasted_iota(jnp.int32, (rows_dev, tile_size), 1)
    above = jnp.logical_and((row_tile == col_tile)[:, None, None], (row_inside < col_inside)[None])
    pieces = jnp.where(above, jnp.float32(0.0), pieces)
    tile_index = jnp.where(valid, row_tile * (row_tile + 1) // 2 + col_tile, 0)
    target = jnp.where(valid, tile_owner[tile_index] % count_y, count_y)
    earlier = jnp.logical_and(
        target[:, None] == target[None, :], tile_index[None, :] < tile_index[:, None]
    )
    earlier = jnp.logical_and(earlier, valid[None, :])
    rank = jnp.sum(earlier.astype(jnp.int32), axis=1)
    outgoing = jnp.zeros((count_y, capacity, rows_dev, tile_size), jnp.float32)
    outgoing = outgoing.at[target, rank].set(pieces, mode="drop")
    incoming = lax.all_to_all(outgoing, "gy", split_axis=0, concat_axis=0, tiled=True)
    my_index = x_index * count_y + y_index
    inverse = jnp.full((devices * slot_count,), lower_count, jnp.int32)
    inverse = inverse.at[tile_owner * slot_count + tile_slot].set(
        jnp.arange(lower_count, dtype=jnp.int32)
    )
    my_tiles = lax.dynamic_slice_in_dim(inverse, my_index * slot_count, slot_count, 0)
    present = my_tiles < lower_count
    clipped = jnp.minimum(my_tiles, lower_count - 1)
    lower_i, lower_j = np.tril_indices(tile_count)
    my_rows = jnp.asarray(lower_i, jnp.int32)[clipped]
    my_cols = jnp.asarray(lower_j, jnp.int32)[clipped]
    class_r, my_rowwise = classify(my_rows, my_cols, half_tiles, count_x)
    before = jnp.logical_and(
        class_r[:, None] == class_r[None, :], clipped[None, :] < clipped[:, None]
    )
    before = jnp.logical_and(before, present[None, :])
    my_rank = jnp.minimum(jnp.sum(before.astype(jnp.int32), axis=1), capacity - 1)
    upper_half = incoming[2 * class_r, my_rank]
    lower_half = incoming[2 * class_r + 1, my_rank]
    joined = jnp.concatenate([upper_half, lower_half], axis=1)
    assembled = jnp.where(my_rowwise[:, None, None], joined, jnp.swapaxes(joined, 1, 2))
    return jnp.where(present[:, None, None], assembled, jnp.float32(0.0))


def solution(mesh):
    placed = (P(("gx", "gy"), None), P(), P())
    return jax.shard_map(
        per_device,
        mesh=mesh,
        in_specs=placed,
        out_specs=P(("gx", "gy"), None, None),
        check_vma=False,
    )
```

profile of v0, /device:TPU:0, one launch (start us, length us, event | category | flops | bytes accessed | tf_op | source)
XLA Modules:
  0.0 106.3 jit_solution(15832038358745648112)
XLA Ops:
  6.5 0.0 copy-start.2
  6.5 0.0 all-gather.2.cloned.1.call-start
  6.5 0.7 all-gather.2.cloned.1.call-update
  7.3 3.1 %collective-permute-start = (f32[128,1024]{1,0:T(8,128)}, f32[128,1024]{1,0:T(8,128)S(1)}, u32[]{:S(2)}, u32[]{:S(2)}) collective-permute-start(f32[128,1024]{1,0:T(8,128)} %param.6), channel_id=1, source_target_pairs={{0,8},{8,16},{16,24},{24,0},{1,9},{9,17},{17,25},{25,1},{2,10},{10... | collective-permute-start | bytes 1572872 | tf_op jit(solution)/shard_map/ppermute | solution.py:11
  10.4 2.6 %collective-permute-start.1 = (f32[128,1024]{1,0:T(8,128)}, f32[128,1024]{1,0:T(8,128)S(1)}, u32[]{:S(2)}, u32[]{:S(2)}) collective-permute-start(f32[128,1024]{1,0:T(8,128)} %param.6), channel_id=1, source_target_pairs={{0,16},{8,24},{16,0},{24,8},{1,17},{9,25},{17,1},{25,9},{2,18},{10... | collective-permute-start | bytes 1572872 | tf_op jit(solution)/shard_map/ppermute | solution.py:11
  13.0 0.7 compare_select_fusion
  13.7 1.0 scatter_custom_fusion
  14.7 0.1 compare_select_fusion.8
  14.8 0.8 fusion.35
  15.6 1.3 %gather_fusion.2 = s32[9]{0:T(128)S(1)} fusion(s32[136]{0:T(256)} %param.7, s32[1024]{0:T(1024)S(1)} %get-tuple-element.16), kind=kCustom, calls=%fused_computation.2 | custom fusion | bytes 108 | tf_op jit(solution)/shard_map/gather | solution.py:86
  17.0 0.2 convert_reduce_fusion
  17.2 0.7 fusion.19
  17.9 0.1 iota_compare_fusion
  18.0 7.4 %collective-permute-done = f32[128,1024]{1,0:T(8,128)S(1)} collective-permute-done((f32[128,1024]{1,0:T(8,128)}, f32[128,1024]{1,0:T(8,128)S(1)}, u32[]{:S(2)}, u32[]{:S(2)}) %collective-permute-start) | collective-permute-done | bytes 524320 | tf_op jit(solution)/shard_map/ppermute | solution.py:11
  25.5 21.5 %collective-permute-done.1 = f32[128,1024]{1,0:T(8,128)S(1)} collective-permute-done((f32[128,1024]{1,0:T(8,128)}, f32[128,1024]{1,0:T(8,128)S(1)}, u32[]{:S(2)}, u32[]{:S(2)}) %collective-permute-start.1) | collective-permute-done | bytes 524320 | tf_op jit(solution)/shard_map/ppermute | solution.py:11
  47.0 1.6 %all-gather.2.cloned.1.call-done = f32[1024,1024]{1,0:T(8,128)} async-done(((f32[128,1024]{1,0:T(8,128)}), f32[1024,1024]{1,0:T(8,128)}) %all-gather.2.cloned.1.call-update) | async-done | bytes 4194320 | tf_op jit(solution)/shard_map/all_gather | solution.py:71
  48.6 0.0 copy-done.2
  48.6 7.3 %fusion = f32[3,128,1024]{2,1,0:T(8,128)S(1)} fusion(f32[1024,1024]{1,0:T(8,128)} %all-gather.2.cloned.1.call-done, f32[1,128,1024]{2,1,0:T(8,128)S(1)} %bitcast.84, f32[1,128,1024]{2,1,0:T(8,128)S(1)} %bitcast.83, f32[1,128,1024]{2,1,0:T(8,128)S(1)} %bitcast.82), kind=kOutput, calls=%fused_computation.8 | convolution fusion | flops 4832624640 | bytes 7340032 | tf_op jit(solution)/shard_map/srk,ck->src/dot_general | solution.py:68
  55.9 0.2 copy.14
  56.0 0.6 gather_fusion.3
  56.7 0.2 and_select_fusion
  56.9 1.6 %broadcast_in_dim.74 = f32[8,2,128,256]{3,2,1,0:T(8,128)} broadcast(f32[]{:T(128)} %constant.161.clone.1), dimensions={} | broadcast | bytes 2097156 | tf_op jit(solution)/shard_map/broadcast_in_dim | solution.py:92
  58.5 3.8 %scatter_fusion = f32[8,2,128,256]{3,2,1,0:T(8,128)} fusion(f32[8,2,128,256]{3,2,1,0:T(8,128)} %broadcast_in_dim.74, s32[9]{0:T(128)S(1)} %fusion.30, f32[9,128,256]{2,1,0:T(8,128)S(1)} %and_select_fusion), kind=kCustom, calls=%fused_computation.7 | custom fusion | bytes 3539016 | tf_op jit(solution)/shard_map/scatter | solution.py:93
  62.3 0.0 copy-start.1
  62.3 0.0 copy-start
  62.3 3.7 %all-to-all-start = ((f32[8,2,128,256]{3,2,1,0:T(8,128)}), f32[8,2,128,256]{3,2,1,0:T(8,128)S(1)}, u32[]{:S(2)}, u32[]{:S(2)}) async-start(f32[8,2,128,256]{3,2,1,0:T(8,128)} %scatter_fusion), calls=%async_computation | async-start | bytes 4194304 | tf_op jit(solution)/shard_map/all_to_all | solution.py:94
  66.0 0.0 copy-done.1
  66.0 0.6 gather_fusion
  66.7 0.0 copy-done
  66.7 0.7 gather_fusion.1
  67.3 0.1 broadcast_compare_fusion
  67.4 0.2 convert_reduce_fusion.1
  67.6 24.9 %all-to-all-done = f32[8,2,128,256]{3,2,1,0:T(8,128)S(1)} async-done(((f32[8,2,128,256]{3,2,1,0:T(8,128)}), f32[8,2,128,256]{3,2,1,0:T(8,128)S(1)}, u32[]{:S(2)}, u32[]{:S(2)}) %all-to-all-start) | async-done | bytes 2097184 | tf_op jit(solution)/shard_map/all_to_all | solution.py:94
  92.5 1.5 %gather_fusion.4 = f32[5,128,256]{2,1,0:T(8,128)} fusion(f32[8,2,128,256]{3,2,1,0:T(8,128)S(1)} %all-to-all-done, s32[5]{0:T(128)S(1)} %get-tuple-element.15), kind=kCustom, calls=%fused_computation.4 | custom fusion | bytes 1310760 | tf_op jit(solution)/shard_map/gather | solution.py:112
  94.0 1.1 %constant_dynamic-update-slice_fusion.1 = f32[5,256,256]{2,1,0:T(8,128)S(1)} fusion(f32[5,128,256]{2,1,0:T(8,128)} %gather_fusion.4), kind=kLoop, calls=%fused_computation.24 | loop fusion | bytes 1310720
  95.1 1.5 %gather_fusion.5 = f32[5,128,256]{2,1,0:T(8,128)} fusion(f32[8,2,128,256]{3,2,1,0:T(8,128)S(1)} %all-to-all-done, s32[5]{0:T(128)S(1)} %get-tuple-element.14), kind=kCustom, calls=%fused_computation.5 | custom fusion | bytes 1310760 | tf_op jit(solution)/shard_map/gather | solution.py:113
  96.6 1.1 %constant_dynamic-update-slice_fusion = f32[5,256,256]{2,1,0:T(8,128)S(1)} fusion(f32[5,256,256]{2,1,0:T(8,128)S(1)} %constant_dynamic-update-slice_fusion.1, f32[5,128,256]{2,1,0:T(8,128)} %gather_fusion.5), kind=kLoop, calls=%fused_computation.23 | loop fusion | bytes 1310720 | tf_op jit(solution)/shard_map/concatenate | solution.py:114
  97.7 0.4 copy.11
  98.1 1.3 %fusion.7 = f32[5,256,256]{2,1,0:T(8,128)} fusion(f32[5,256,256]{2,1,0:T(8,128)S(1)} %constant_dynamic-update-slice_fusion, f32[5,256,256]{1,2,0:T(8,128)S(1)} %copy.11, pred[5]{0:T(512)(128)(4,1)S(1)} %get-tuple-element.6, pred[5]{0:T(512)(128)(4,1)S(1)} %broadcast_compare_fusion), kind=kLoop, calls=%fused_computation.17 | loop fusion | flops 655360 | bytes 3932170 | tf_op jit(solution)/shard_map/jit(_where)/select_n | solution.py:116
  (16 shorter events, 0.2 us)
Async XLA Ops:
  6.5 42.0 %copy-start.2 = (f32[128,1024]{1,0:T(8,128)S(1)}, f32[128,1024]{1,0:T(8,128)}, u32[]{:S(2)}) copy-start(f32[128,1024]{1,0:T(8,128)} %param.6) | copy-start | bytes 1572868
  6.5 42.0 %all-gather.2.cloned.1.call-start = ((), (), s32[]{:S(2)}) async-start(), calls=%async_computation.1 | async-start | bytes 4718592 | tf_op jit(solution)/shard_map/all_gather | solution.py:71
  7.3 18.2 %collective-permute-start = (f32[128,1024]{1,0:T(8,128)}, f32[128,1024]{1,0:T(8,128)S(1)}, u32[]{:S(2)}, u32[]{:S(2)}) collective-permute-start(f32[128,1024]{1,0:T(8,128)} %param.6), channel_id=1, source_target_pairs={{0,8},{8,16},{16,24},{24,0},{1,9},{9,17},{17,25},{25,1},{2,10},{10... | collective-permute-start | bytes 1572872 | tf_op jit(solution)/shard_map/ppermute | solution.py:11
  10.4 36.6 %collective-permute-start.1 = (f32[128,1024]{1,0:T(8,128)}, f32[128,1024]{1,0:T(8,128)S(1)}, u32[]{:S(2)}, u32[]{:S(2)}) collective-permute-start(f32[128,1024]{1,0:T(8,128)} %param.6), channel_id=1, source_target_pairs={{0,16},{8,24},{16,0},{24,8},{1,17},{9,25},{17,1},{25,9},{2,18},{10... | collective-permute-start | bytes 1572872 | tf_op jit(solution)/shard_map/ppermute | solution.py:11
  62.3 3.7 %copy-start.1 = (s32[136]{0:T(256)S(1)}, s32[136]{0:T(256)}, u32[]{:S(2)}) copy-start(s32[136]{0:T(256)} %constant.167.clone) | copy-start | bytes 1636
  62.3 4.4 %copy-start = (s32[136]{0:T(256)S(1)}, s32[136]{0:T(256)}, u32[]{:S(2)}) copy-start(s32[136]{0:T(256)} %constant.168.clone) | copy-start | bytes 1636
  62.3 30.3 %all-to-all-start = ((f32[8,2,128,256]{3,2,1,0:T(8,128)}), f32[8,2,128,256]{3,2,1,0:T(8,128)S(1)}, u32[]{:S(2)}, u32[]{:S(2)}) async-start(f32[8,2,128,256]{3,2,1,0:T(8,128)} %scatter_fusion), calls=%async_computation | async-start | bytes 4194304 | tf_op jit(solution)/shard_map/all_to_all | solution.py:94
Sparse Core Ops, SparseCore 0:
  9.2 39.2 all-gather.1
where the time goes:
time: 107 us; the launch traced here: 106 us
  waiting for transfers between devices  56.1 us (52%)
  local copies, waits for them, and re-layouts  15.4 us (14%)
  between operations  13.6 us (13%)
  starting transfers between devices  9.43 us (9%)
  matrix products  7.3 us (7%)
  other arithmetic  4.43 us (4%)
    ppermute x2, waiting for transfers between devices, from_behind(): return lax.ppermute(value, axis, pairs)  29 us
    all_to_all x1, waiting for transfers between devices, per_device(): lax.all_to_all(outgoing, 'gy', split_axis=0, concat_axis=0, tiled=True)  24.9 us
    dot_general x1, matrix products, per_device(): jnp.einsum('srk,ck->src', stacked, lax.all_gather(matrix_rows, 'gy', axis...  7.3 us
    ppermute x2, starting transfers between devices, from_behind(): return lax.ppermute(value, axis, pairs)  5.69 us
    scatter x1, local copies, waits for them, and re-layouts, per_device(): outgoing = outgoing.at[target, rank].set(pieces, mode='drop')  3.8 us
    all_to_all x1, starting transfers between devices, per_device(): lax.all_to_all(outgoing, 'gy', split_axis=0, concat_axis=0, tiled=True)  3.73 us
  transfers between devices with their start and end apart: 4, of which 4 were waited for; matrix products, arithmetic and copies ran while one was open for 6% of the time, Pallas kernels for 0%

commit v1 on v0

v1 whole, which is shorter than its diff:
```python
import functools

import jax
import jax.numpy as jnp
from jax import lax
from jax.experimental import pallas as pl
from jax.experimental.pallas import tpu as pltpu
from jax.sharding import PartitionSpec as P

MESH = pl.DeviceIdType.MESH


def chip_position(chip, chips):
    row, col = lax.div(chip, 2), lax.rem(chip, 2)
    return col * (1 + row) + (1 - col) * lax.rem(chips - row, chips)


def chip_at(position, chips):
    behind = lax.rem(position + chips - 1, chips)
    far = lax.div(behind, chips // 2)
    return (1 - far) * (2 * behind + 1) + far * 2 * (chips - 1 - behind)


def piece_lists(half_tiles, half_x):
    lists, start = [], 0
    for step in range(half_x + 1):
        if step == 0:
            count = half_tiles // 2 + 1
        elif step < half_x:
            count = half_tiles
        else:
            count = half_tiles // 2
        lists.append((step, start, count))
        start += count
    return lists, start


def piece(x, r, step, i, nx, half_tiles, half_x):
    source = lax.rem(x - step + nx, nx)
    if step == 0:
        col = lax.rem(r - i + half_tiles, half_tiles)
        valid = jnp.logical_or(i < half_tiles // 2, r < half_tiles // 2)
        rowwise = col <= r
    elif step < half_x:
        col = i
        valid = i >= 0
        rowwise = source > x
    else:
        flag = jnp.where(x >= half_x, 1, 0)
        col = 2 * i + lax.rem(r + flag, 2)
        valid = i >= 0
        rowwise = source > x
    other, mine = source * half_tiles + r, x * half_tiles + col
    row_tile = jnp.where(rowwise, other, mine)
    col_tile = jnp.where(rowwise, mine, other)
    tile = jnp.where(valid, row_tile * (row_tile + 1) // 2 + col_tile, 0)
    return col, valid, rowwise, tile


def kernel(
    dims, rows_ref, owner_ref, slot_ref, out_ref,
    gath, zbuf, chi, clo, zhi, zlo, pieces, outgoing, incoming, targets,
    gs_r, gr_r, gs_l, gr_l, ss, sr, zs, zr, xs, xr,
):
    nx, ny, half_tiles, half_x, capacity, slots = dims
    rows = rows_ref.shape[0]
    half = rows // 2
    chips = ny // 2
    reach = chips // 2
    x = lax.axis_index("gx")
    y = lax.axis_index("gy")
    core = lax.rem(y, 2)
    chip = lax.div(y, 2)
    right_x, left_x = lax.rem(x + 1, nx), lax.rem(x + nx - 1, nx)
    sibling = y + 1 - 2 * core
    place = chip_position(chip, chips)

    def at(position):
        return 2 * chip_at(lax.rem(position + chips, chips), chips) + core

    next_y, prev_y = at(place + 1), at(place - 1)
    lists, piece_count = piece_lists(half_tiles, half_x)

    barrier = pltpu.get_barrier_semaphore()
    for other in (right_x, left_x):
        pl.semaphore_signal(barrier, inc=1, device_id=(other, y), device_id_type=MESH)
    for offset in range(1, ny):
        pl.semaphore_signal(
            barrier, inc=1, device_id=(x, lax.rem(y + offset, ny)), device_id_type=MESH
        )
    pl.semaphore_wait(barrier, ny + 1)

    started = []

    def send(src, dst, send_sem, recv_sem, target):
        copy = pltpu.make_async_remote_copy(
            src_ref=src, dst_ref=dst, send_sem=send_sem, recv_sem=recv_sem,
            device_id=target, device_id_type=MESH,
        )
        copy.start()
        started.append(copy)

    def part(h):
        return pl.ds(h * half, half)

    def zcopy(step, h):
        src = rows_ref.at[part(h)] if step == 1 else zbuf.at[step - 2, part(h)]
        send(src, zbuf.at[step - 1, part(h)], zs.at[step - 1, h], zr.at[step - 1, h], (right_x, y))

    def block(owner, h):
        return gath.at[owner, part(h)]

    def ring(direction, distance, h):
        owner = at(place - direction * (distance - 1))
        src = rows_ref.at[part(h)] if distance == 1 else block(owner, h)
        s, r = (gs_r, gr_r) if direction == 1 else (gs_l, gr_l)
        target = next_y if direction == 1 else prev_y
        send(src, block(owner, h), s.at[distance - 1, h], r.at[distance - 1, h], (x, target))

    def cross(number, owner, h):
        src = rows_ref.at[part(h)] if number == 0 else block(owner, h)
        send(src, block(owner, h), ss.at[number, h], sr.at[number, h], (x, sibling))

    def halves_of(direction, distance):
        if distance < reach:
            return (0, 1) if direction == 1 else (1, 0)
        return (0,) if direction == 1 else (1,)

    def split(value, hi_ref, lo_ref, index):
        hi = value.astype(jnp.bfloat16)
        hi_ref[index] = hi
        lo_ref[index] = (value - hi.astype(jnp.float32)).astype(jnp.bfloat16)

    zcopy(1, 0)
    ring(1, 1, 0)
    if reach > 1:
        ring(-1, 1, 1)
        zcopy(1, 1)
        ring(1, 1, 1)
        ring(-1, 1, 0)
    else:
        ring(-1, 1, 1)
        zcopy(1, 1)
    cross(0, y, 0)
    cross(0, y, 1)

    for step, first, count in lists:
        def fill(i, carry, step=step, first=first):
            _, valid, _, tile = piece(x, chip, step, i, nx, half_tiles, half_x)
            targets[first + i] = jnp.where(valid, lax.rem(owner_ref[tile], ny), ny)
            return carry
        lax.fori_loop(0, count, fill, 0)

    me = x * ny + y

    def class_loop(r, carry):
        state = (jnp.int32(0),) + carry
        for step, first, count in lists:
            def look(i, state, step=step):
                seen, found = state[0], state[1:]
                _, valid, rowwise, tile = piece(x, r, step, i, nx, half_tiles, half_x)
                mine = jnp.where(valid, jnp.where(owner_ref[tile] == me, 1, 0), 0)
                slot = slot_ref[tile]
                code = 2 * (r * capacity + jnp.minimum(seen, capacity - 1))
                code = code + jnp.where(rowwise, 1, 0)
                key = jnp.where(mine == 1, slot, slots)
                found = tuple(jnp.where(key == s, code, found[s]) for s in range(slots))
                return (seen + mine,) + found
            state = lax.fori_loop(0, count, look, state)
        return state[1:]

    found = lax.fori_loop(0, half_tiles, class_loop, (jnp.int32(-1),) * slots)

    chosen = []
    for offset in range(ny):
        dest = lax.rem(y + offset, ny)

        def pick(p, state, dest=dest):
            hit = jnp.where(targets[p] == dest, 1, 0)
            seen = state[0]
            key = jnp.where(hit == 1, seen, capacity)
            picks = tuple(jnp.where(key == k, p, state[1 + k]) for k in range(capacity))
            return (seen + hit,) + picks

        chosen.append(lax.fori_loop(0, piece_count, pick, (jnp.int32(0),) * (capacity + 1))[1:])

    def wait_recv(dst, sem):
        pltpu.make_async_remote_copy(
            src_ref=dst, dst_ref=dst, send_sem=sem, recv_sem=sem,
            device_id=(x, sibling), device_id_type=MESH,
        ).wait_recv()

    split(rows_ref[...], zhi, zlo, 0)
    split(rows_ref[...], chi, clo, y)

    def take_cross(number, owner, halves):
        for h in halves:
            wait_recv(block(owner, h), sr.at[number, h])

    number = 1
    pending = [(0, sibling, (0, 1))]
    for distance in range(1, reach + 1):
        if distance <= half_x:
            for h in (0, 1):
                wait_recv(zbuf.at[distance - 1, part(h)], zr.at[distance - 1, h])
                if distance < half_x:
                    zcopy(distance + 1, h)
                if h in halves_of(1, distance):
                    owner = at(place - distance)
                    wait_recv(block(owner, h), gr_r.at[distance - 1, h])
                    if distance < reach and h in halves_of(1, distance + 1):
                        ring(1, distance + 1, h)
                    cross(2 * distance - 1, owner, h)
                g = 1 - h
                if g in halves_of(-1, distance):
                    owner = at(place + distance)
                    wait_recv(block(owner, g), gr_l.at[distance - 1, g])
                    if distance < reach and g in halves_of(-1, distance + 1):
                        ring(-1, distance + 1, g)
                    cross(2 * distance, owner, g)
            split(zbuf[distance - 1], zhi, zlo, distance)
        behind, ahead = at(place - distance), at(place + distance)
        pending.append((2 * distance - 1, behind + 1 - 2 * core, halves_of(1, distance)))
        pending.append((2 * distance, ahead + 1 - 2 * core, halves_of(-1, distance)))
        split(gath[behind], chi, clo, behind)
        if distance < reach:
            split(gath[ahead], chi, clo, ahead)
        for number, owner, halves in pending[: (1 if distance == 1 else 0)]:
            take_cross(number, owner, halves)
            split(gath[owner], chi, clo, owner)
    for number, owner, halves in pending[1:-2]:
        take_cross(number, owner, halves)
        split(gath[owner], chi, clo, owner)
    for number, owner, halves in pending[-2:]:
        take_cross(number, owner, halves)
    split(gath[pending[-1][1]], chi, clo, pending[-1][1])
    for step in range(reach + 1, half_x + 1):
        for h in (0, 1):
            wait_recv(zbuf.at[step - 1, part(h)], zr.at[step - 1, h])
            if step < half_x:
                zcopy(step + 1, h)
        split(zbuf[step - 1], zhi, zlo, step)

    def mul(a_hi, a_lo, b_hi, b_lo):
        dims_nt = (((1,), (1,)), ((), ()))
        one = functools.partial(
            lax.dot_general, dimension_numbers=dims_nt, preferred_element_type=jnp.float32
        )
        return one(a_hi, b_hi) + (one(a_hi, b_lo) + one(a_lo, b_hi))

    width = rows_ref.shape[1]
    row_inside = core * rows + lax.broadcasted_iota(jnp.int32, (rows, 2 * rows), 0)
    col_inside = lax.broadcasted_iota(jnp.int32, (rows, 2 * rows), 1)
    above = jnp.where(row_inside < col_inside, 1, 0)
    for step, first, count in lists:
        def make(i, carry, step=step, first=first):
            col, _, rowwise, _ = piece(x, chip, step, i, nx, half_tiles, half_x)
            a_hi, a_lo = zhi[step], zlo[step]
            b_hi = chi[pl.ds(2 * col, 2)].reshape(2 * rows, width)
            b_lo = clo[pl.ds(2 * col, 2)].reshape(2 * rows, width)

            @pl.when(rowwise)
            def _():
                full = mul(a_hi, a_lo, b_hi, b_lo)
                if step == 0:
                    full = jnp.where(above * jnp.where(i == 0, 1, 0) == 1, 0.0, full)
                pieces[first + i, 0] = full[:, :rows]
                pieces[first + i, 1] = full[:, rows:]

            @pl.when(jnp.logical_not(rowwise))
            def _():
                full = mul(b_hi, b_lo, a_hi, a_lo)
                pieces[first + i, 0] = full[:rows]
                pieces[first + i, 1] = full[rows:]

            return carry
        lax.fori_loop(0, count, make, 0)

    def arrival(offset):
        return pl.ds(offset * capacity * 2, capacity * 2)

    def exchange(offset):
        dest = lax.rem(y + offset, ny)
        send(
            outgoing.at[offset], incoming.at[arrival(offset)],
            xs.at[offset], xr.at[offset], (x, dest),
        )

    order = [o for o in range(1, ny)]
    for n, offset in enumerate(order):
        for k in range(capacity):
            outgoing[offset, 2 * k:2 * k + 2] = pieces[chosen[offset][k]]
        if n > 0:
            exchange(order[n - 1])
    for k in range(capacity):
        incoming[2 * k:2 * k + 2] = pieces[chosen[0][k]]
    exchange(order[-1])
    for offset in range(1, ny):
        wait_recv(incoming.at[arrival(offset)], xr.at[offset])

    for s in range(slots):
        code = found[s]
        there = code >= 0
        safe = jnp.maximum(code, 0)
        rowwise = lax.rem(safe, 2) == 1
        rank = lax.rem(safe // 2, capacity)
        first_source = 2 * (safe // (2 * capacity))
        bases = [
            (lax.rem(y - first_source - h + ny, ny) * capacity + rank) * 2 for h in (0, 1)
        ]
        for i in (0, 1):
            for j in (0, 1):
                place_of = jnp.where(rowwise, bases[i] + j, bases[j] + i)
                value = incoming[place_of]
                out_ref[s, i * rows:(i + 1) * rows, j * rows:(j + 1) * rows] = jnp.where(
                    there, value, 0.0
                )
    for copy in started:
        copy.wait_send()


def per_device(mesh_shape, matrix_rows, tile_owner, tile_slot):
    nx, ny = mesh_shape
    rows, width = matrix_rows.shape
    half_tiles, half_x = ny // 2, nx // 2
    capacity = nx // 4 + 1
    slots = -(-tile_owner.shape[0] // (nx * ny))
    _, piece_count = piece_lists(half_tiles, half_x)
    reach = max(ny // 4, 1)
    f32, bf16 = jnp.float32, jnp.bfloat16
    dma = pltpu.SemaphoreType.DMA
    return pl.pallas_call(
        functools.partial(kernel, (nx, ny, half_tiles, half_x, capacity, slots)),
        out_shape=jax.ShapeDtypeStruct((slots, 2 * rows, 2 * rows), f32),
        in_specs=[
            pl.BlockSpec(memory_space=pltpu.VMEM),
            pl.BlockSpec(memory_space=pltpu.SMEM),
            pl.BlockSpec(memory_space=pltpu.SMEM),
        ],
        out_specs=pl.BlockSpec(memory_space=pltpu.VMEM),
        scratch_shapes=[
            pltpu.VMEM((ny, rows, width), f32),
            pltpu.VMEM((half_x, rows, width), f32),
            pltpu.VMEM((ny, rows, width), bf16),
            pltpu.VMEM((ny, rows, width), bf16),
            pltpu.VMEM((half_x + 1, rows, width), bf16),
            pltpu.VMEM((half_x + 1, rows, width), bf16),
            pltpu.VMEM((piece_count, 2, rows, rows), f32),
            pltpu.VMEM((ny, 2 * capacity, rows, rows), f32),
            pltpu.VMEM((ny * 2 * capacity, rows, rows), f32),
            pltpu.SMEM((piece_count,), jnp.int32),
            dma((reach, 2)), dma((reach, 2)), dma((reach, 2)), dma((reach, 2)),
            dma((2 * reach + 1, 2)), dma((2 * reach + 1, 2)),
            dma((half_x, 2)), dma((half_x, 2)),
            dma((ny,)), dma((ny,)),
        ],
        compiler_params=pltpu.CompilerParams(
            collective_id=0, has_side_effects=True, vmem_limit_bytes=60 * 1024 * 1024
        ),
    )(matrix_rows, tile_owner, tile_slot)


def solution(mesh):
    placed = (P(("gx", "gy"), None), P(), P())
    return jax.shard_map(
        functools.partial(per_device, (mesh.shape["gx"], mesh.shape["gy"])),
        mesh=mesh,
        in_specs=placed,
        out_specs=P(("gx", "gy"), None, None),
        check_vma=False,
    )
```

time: 107 us -> 66.2 us (0.62)
  Pallas kernels: 0 us -> 62.9 us
  waiting for transfers between devices: 56.1 us -> 0 us
  between operations: 13.6 us -> 0.01 us
  local copies, waits for them, and re-layouts: 15.4 us -> 2.51 us
  starting transfers between devices: 9.43 us -> 0 us
  matrix products: 7.3 us -> 0 us
  other arithmetic: 4.43 us -> 0 us
    pallas_call x0 -> x1, Pallas kernels: none -> 62.9 us  [per_device(): pl.pallas_call(functools.partial(kernel, (nx, ny, half_tiles, half_x, cap...]
    ppermute x2 -> x0, waiting for transfers between devices: 29 us -> none  [from_behind(): return lax.ppermute(value, axis, pairs)]
    all_to_all x1 -> x0, waiting for transfers between devices: 24.9 us -> none  [per_device(): lax.all_to_all(outgoing, 'gy', split_axis=0, concat_axis=0, tiled=True)]
    dot_general x1 -> x0, matrix products: 7.3 us -> none  [per_device(): jnp.einsum('srk,ck->src', stacked, lax.all_gather(matrix_rows, 'gy', axis...]
    gather x6 -> x0, local copies, waits for them, and re-layouts: 6.18 us -> none  [the longest x1 1.46 us: per_device(): lower_half = incoming[2 * class_r + 1, my_rank]]
    ppermute x2 -> x0, starting transfers between devices: 5.69 us -> none  [from_behind(): return lax.ppermute(value, axis, pairs)]
    scatter x2 -> x0, local copies, waits for them, and re-layouts: 4.81 us -> none  [the longest x1 3.8 us: per_device(): outgoing = outgoing.at[target, rank].set(pieces, mode='drop')]
    all_to_all x1 -> x0, starting transfers between devices: 3.73 us -> none  [per_device(): lax.all_to_all(outgoing, 'gy', split_axis=0, concat_axis=0, tiled=True)]
  transfers between devices with their start and end apart: 4 -> 0, of which waited for: 4 -> 0; matrix products, arithmetic and copies ran while one was open for 6% -> 0% of each run, Pallas kernels for 0% -> 0%
where the time goes in v1:
time: 66.2 us; the launch traced here: 65.4 us
  Pallas kernels  62.9 us (95%)
  local copies, waits for them, and re-layouts  2.51 us (4%)
    pallas_call x1, Pallas kernels, per_device(): pl.pallas_call(functools.partial(kernel, (nx, ny, half_tiles, half_x, cap...  62.9 us
    unnamed x1, local copies, waits for them, and re-layouts  2.51 us

profile of v1, /device:TPU:0, one launch (start us, length us, event | category | flops | bytes accessed | tf_op | source)
XLA Modules:
  0.0 65.4 jit_solution(9917608942187973081)
XLA Ops:
  0.0 62.9 %shard_map.37 = f32[5,256,256]{2,1,0:T(8,128)} custom-call(f32[128,1024]{1,0:T(8,128)} %rows_ref.1, s32[136]{0:T(256)} %owner_ref.1, s32[136]{0:T(256)} %slot_ref.1), custom_call_target="tpu_custom_call" | custom-call | tf_op jit(solution)/shard_map/pallas_call | solution.py:332
  62.9 2.5 %copy.5 = f32[5,256,256]{2,1,0:T(8,128)} copy(f32[5,256,256]{2,1,0:T(8,128)} %shard_map.37) | data formatting | bytes 2621440

commit v2 on v1

--- a/solution.py
+++ b/solution.py
@@ -59,7 +59,7 @@
 
 def kernel(
     dims, rows_ref, owner_ref, slot_ref, out_ref,
-    gath, zbuf, chi, clo, zhi, zlo, pieces, outgoing, incoming, targets,
+    gath, zbuf, chi, clo, zsplit, pieces, outgoing, incoming, targets,
     gs_r, gr_r, gs_l, gr_l, ss, sr, zs, zr, xs, xr,
 ):
     nx, ny, half_tiles, half_x, capacity, slots = dims
@@ -190,7 +190,20 @@
             device_id=(x, sibling), device_id_type=MESH,
         ).wait_recv()
 
-    split(rows_ref[...], zhi, zlo, 0)
+    def split_other(step, h):
+        ref = rows_ref.at[part(h)] if step == 0 else zbuf.at[step - 1, part(h)]
+        value = ref[...]
+        hi = value.astype(jnp.bfloat16)
+        zsplit[step, h, :half] = hi
+        zsplit[step, h, half:] = (value - hi.astype(jnp.float32)).astype(jnp.bfloat16)
+
+    def take_other(step, h):
+        wait_recv(zbuf.at[step - 1, part(h)], zr.at[step - 1, h])
+        if step < half_x:
+            zcopy(step + 1, h)
+
+    split_other(0, 0)
+    split_other(0, 1)
     split(rows_ref[...], chi, clo, y)
 
     def take_cross(number, owner, halves):
@@ -202,9 +215,8 @@
     for distance in range(1, reach + 1):
         if distance <= half_x:
             for h in (0, 1):
-                wait_recv(zbuf.at[distance - 1, part(h)], zr.at[distance - 1, h])
-                if distance < half_x:
-                    zcopy(distance + 1, h)
+                if (distance, h) != (half_x, 1):
+                    take_other(distance, h)
                 if h in halves_of(1, distance):
                     owner = at(place - distance)
                     wait_recv(block(owner, h), gr_r.at[distance - 1, h])
@@ -218,7 +230,9 @@
                     if distance < reach and g in halves_of(-1, distance + 1):
                         ring(-1, distance + 1, g)
                     cross(2 * distance, owner, g)
-            split(zbuf[distance - 1], zhi, zlo, distance)
+            split_other(distance, 0)
+            if distance < half_x:
+                split_other(distance, 1)
         behind, ahead = at(place - distance), at(place + distance)
         pending.append((2 * distance - 1, behind + 1 - 2 * core, halves_of(1, distance)))
         pending.append((2 * distance, ahead + 1 - 2 * core, halves_of(-1, distance)))
@@ -236,67 +250,60 @@
     split(gath[pending[-1][1]], chi, clo, pending[-1][1])
     for step in range(reach + 1, half_x + 1):
         for h in (0, 1):
-            wait_recv(zbuf.at[step - 1, part(h)], zr.at[step - 1, h])
-            if step < half_x:
-                zcopy(step + 1, h)
-        split(zbuf[step - 1], zhi, zlo, step)
-
-    def mul(a_hi, a_lo, b_hi, b_lo):
-        dims_nt = (((1,), (1,)), ((), ()))
-        one = functools.partial(
-            lax.dot_general, dimension_numbers=dims_nt, preferred_element_type=jnp.float32
-        )
-        return one(a_hi, b_hi) + (one(a_hi, b_lo) + one(a_lo, b_hi))
-
+            if (step, h) != (half_x, 1):
+                take_other(step, h)
+                split_other(step, h)
+
+    one = functools.partial(
+        lax.dot_general,
+        dimension_numbers=(((1,), (1,)), ((), ())),
+        preferred_element_type=jnp.float32,
+    )
     width = rows_ref.shape[1]
-    row_inside = core * rows + lax.broadcasted_iota(jnp.int32, (rows, 2 * rows), 0)
-    col_inside = lax.broadcasted_iota(jnp.int32, (rows, 2 * rows), 1)
-    above = jnp.where(row_inside < col_inside, 1, 0)
-    for step, first, count in lists:
-        def make(i, carry, step=step, first=first):
-            col, _, rowwise, _ = piece(x, chip, step, i, nx, half_tiles, half_x)
-            a_hi, a_lo = zhi[step], zlo[step]
-            b_hi = chi[pl.ds(2 * col, 2)].reshape(2 * rows, width)
-            b_lo = clo[pl.ds(2 * col, 2)].reshape(2 * rows, width)
-
-            @pl.when(rowwise)
-            def _():
-                full = mul(a_hi, a_lo, b_hi, b_lo)
+    row_inside = core * rows + lax.broadcasted_iota(jnp.int32, (half, 2 * rows), 0)
+    col_inside = lax.broadcasted_iota(jnp.int32, (half, 2 * rows), 1)
+
+    def multiply(h):
+        above = jnp.where(row_inside + h * half < col_inside, 1, 0)
+        for step, first, count in lists:
+            def make(i, carry, step=step, first=first):
+                col, _, _, _ = piece(x, chip, step, i, nx, half_tiles, half_x)
+                b_hi = chi[pl.ds(2 * col, 2)].reshape(2 * rows, width)
+                b_lo = clo[pl.ds(2 * col, 2)].reshape(2 * rows, width)
+                both = one(zsplit[step, h], b_hi)
+                full = both[:half] + (both[half:] + one(zsplit[step, h, :half], b_lo))
                 if step == 0:
                     full = jnp.where(above * jnp.where(i == 0, 1, 0) == 1, 0.0, full)
-                pieces[first + i, 0] = full[:, :rows]
-                pieces[first + i, 1] = full[:, rows:]
-
-            @pl.when(jnp.logical_not(rowwise))
-            def _():
-                full = mul(b_hi, b_lo, a_hi, a_lo)
-                pieces[first + i, 0] = full[:rows]
-                pieces[first + i, 1] = full[rows:]
-
-            return carry
-        lax.fori_loop(0, count, make, 0)
+                pieces[h, first + i, 0] = full[:, :rows]
+                pieces[h, first + i, 1] = full[:, rows:]
+                return carry
+            lax.fori_loop(0, count, make, 0)
 
     def arrival(offset):
         return pl.ds(offset * capacity * 2, capacity * 2)
 
-    def exchange(offset):
-        dest = lax.rem(y + offset, ny)
+    def exchange(h, offset):
         send(
-            outgoing.at[offset], incoming.at[arrival(offset)],
-            xs.at[offset], xr.at[offset], (x, dest),
+            outgoing.at[h, offset], incoming.at[h, arrival(offset)],
+            xs.at[h, offset], xr.at[h, offset], (x, lax.rem(y + offset, ny)),
         )
 
-    order = [o for o in range(1, ny)]
-    for n, offset in enumerate(order):
+    for h in (0, 1):
+        if h == 1:
+            take_other(half_x, 1)
+            split_other(half_x, 1)
+        multiply(h)
+        for offset in range(1, ny):
+            for k in range(capacity):
+                outgoing[h, offset, 2 * k:2 * k + 2] = pieces[h, chosen[offset][k]]
+            if offset > 1:
+                exchange(h, offset - 1)
         for k in range(capacity):
-            outgoing[offset, 2 * k:2 * k + 2] = pieces[chosen[offset][k]]
-        if n > 0:
-            exchange(order[n - 1])
-    for k in range(capacity):
-        incoming[2 * k:2 * k + 2] = pieces[chosen[0][k]]
-    exchange(order[-1])
-    for offset in range(1, ny):
-        wait_recv(incoming.at[arrival(offset)], xr.at[offset])
+            incoming[h, 2 * k:2 * k + 2] = pieces[h, chosen[0][k]]
+        exchange(h, ny - 1)
+    for h in (0, 1):
+        for offset in range(1, ny):
+            wait_recv(incoming.at[h, arrival(offset)], xr.at[h, offset])
 
     for s in range(slots):
         code = found[s]
@@ -311,7 +318,8 @@
         for i in (0, 1):
             for j in (0, 1):
                 place_of = jnp.where(rowwise, bases[i] + j, bases[j] + i)
-                value = incoming[place_of]
+                value = jnp.concatenate([incoming[0, place_of], incoming[1, place_of]], axis=0)
+                value = jnp.where(rowwise, value, value.T)
                 out_ref[s, i * rows:(i + 1) * rows, j * rows:(j + 1) * rows] = jnp.where(
                     there, value, 0.0
                 )
@@ -343,16 +351,15 @@
             pltpu.VMEM((half_x, rows, width), f32),
             pltpu.VMEM((ny, rows, width), bf16),
             pltpu.VMEM((ny, rows, width), bf16),
-            pltpu.VMEM((half_x + 1, rows, width), bf16),
-            pltpu.VMEM((half_x + 1, rows, width), bf16),
-            pltpu.VMEM((piece_count, 2, rows, rows), f32),
-            pltpu.VMEM((ny, 2 * capacity, rows, rows), f32),
-            pltpu.VMEM((ny * 2 * capacity, rows, rows), f32),
+            pltpu.VMEM((half_x + 1, 2, rows, width), bf16),
+            pltpu.VMEM((2, piece_count, 2, rows // 2, rows), f32),
+            pltpu.VMEM((2, ny, 2 * capacity, rows // 2, rows), f32),
+            pltpu.VMEM((2, ny * 2 * capacity, rows // 2, rows), f32),
             pltpu.SMEM((piece_count,), jnp.int32),
             dma((reach, 2)), dma((reach, 2)), dma((reach, 2)), dma((reach, 2)),
             dma((2 * reach + 1, 2)), dma((2 * reach + 1, 2)),
             dma((half_x, 2)), dma((half_x, 2)),
-            dma((ny,)), dma((ny,)),
+            dma((2, ny)), dma((2, ny)),
         ],
         compiler_params=pltpu.CompilerParams(
             collective_id=0, has_side_effects=True, vmem_limit_bytes=60 * 1024 * 1024

time: 66.2 us -> 60.5 us (0.914)
  Pallas kernels: 62.9 us -> 56.8 us
    pallas_call x1, Pallas kernels: 62.9 us -> 56.8 us  [per_device(): pl.pallas_call(functools.partial(kernel, (nx, ny, half_tiles, half_x, cap...]
where the time goes in v2:
time: 60.5 us; the launch traced here: 59.3 us
  Pallas kernels  56.8 us (94%)
  local copies, waits for them, and re-layouts  2.51 us (4%)
    pallas_call x1, Pallas kernels, per_device(): pl.pallas_call(functools.partial(kernel, (nx, ny, half_tiles, half_x, cap...  56.8 us
    unnamed x1, local copies, waits for them, and re-layouts  2.51 us

profile of v2, /device:TPU:0, one launch (start us, length us, event | category | flops | bytes accessed | tf_op | source)
XLA Modules:
  0.0 59.3 jit_solution(17840631694277449453)
XLA Ops:
  0.0 56.8 %shard_map.37 = f32[5,256,256]{2,1,0:T(8,128)} custom-call(f32[128,1024]{1,0:T(8,128)} %rows_ref.1, s32[136]{0:T(256)} %owner_ref.1, s32[136]{0:T(256)} %slot_ref.1), custom_call_target="tpu_custom_call" | custom-call | tf_op jit(solution)/shard_map/pallas_call | solution.py:340
  56.8 2.5 %copy.5 = f32[5,256,256]{2,1,0:T(8,128)} copy(f32[5,256,256]{2,1,0:T(8,128)} %shard_map.37) | data formatting | bytes 2621440

commit v3 on v2

--- a/solution.py
+++ b/solution.py
@@ -210,9 +210,56 @@
         for h in halves:
             wait_recv(block(owner, h), sr.at[number, h])
 
-    number = 1
+    one = functools.partial(
+        lax.dot_general,
+        dimension_numbers=(((1,), (1,)), ((), ())),
+        preferred_element_type=jnp.float32,
+    )
+    width = rows_ref.shape[1]
+    row_inside = core * rows + lax.broadcasted_iota(jnp.int32, (half, 2 * rows), 0)
+    col_inside = lax.broadcasted_iota(jnp.int32, (half, 2 * rows), 1)
+
+    def one_piece_of(h):
+        above = jnp.where(row_inside + h * half < col_inside, 1, 0)
+
+        def one_piece(i, step, first, col):
+            b_hi = chi[pl.ds(2 * col, 2)].reshape(2 * rows, width)
+            b_lo = clo[pl.ds(2 * col, 2)].reshape(2 * rows, width)
+            both = one(zsplit[step, h], b_hi)
+            full = both[:half] + (both[half:] + one(zsplit[step, h, :half], b_lo))
+            if step == 0:
+                full = jnp.where(above * jnp.where(i == 0, 1, 0) == 1, 0.0, full)
+            pieces[h, first + i, 0] = full[:, :rows]
+            pieces[h, first + i, 1] = full[:, rows:]
+
+        return one_piece
+
+    farthest = chip_at(lax.rem(place + reach, chips), chips)
+    soon = min(reach, half_x) if reach > 1 else 0
+
+    def multiply(h, mode):
+        one_piece = one_piece_of(h)
+        for step, first, count in lists:
+            if mode == "early" and step >= soon:
+                continue
+
+            def make(i, carry, step=step, first=first):
+                col, _, _, _ = piece(x, chip, step, i, nx, half_tiles, half_x)
+                if mode == "all" or step >= soon:
+                    one_piece(i, step, first, col)
+                else:
+                    wanted = (col != farthest) if mode == "early" else (col == farthest)
+                    pl.when(wanted)(lambda: one_piece(i, step, first, col))
+                return carry
+            lax.fori_loop(0, count, make, 0)
+
     pending = [(0, sibling, (0, 1))]
     for distance in range(1, reach + 1):
+        if distance == reach:
+            for number, owner, halves in pending[1:]:
+                take_cross(number, owner, halves)
+                split(gath[owner], chi, clo, owner)
+            multiply(0, "early")
         if distance <= half_x:
             for h in (0, 1):
                 if (distance, h) != (half_x, 1):
@@ -242,9 +289,6 @@
         for number, owner, halves in pending[: (1 if distance == 1 else 0)]:
             take_cross(number, owner, halves)
             split(gath[owner], chi, clo, owner)
-    for number, owner, halves in pending[1:-2]:
-        take_cross(number, owner, halves)
-        split(gath[owner], chi, clo, owner)
     for number, owner, halves in pending[-2:]:
         take_cross(number, owner, halves)
     split(gath[pending[-1][1]], chi, clo, pending[-1][1])
@@ -254,31 +298,6 @@
                 take_other(step, h)
                 split_other(step, h)
 
-    one = functools.partial(
-        lax.dot_general,
-        dimension_numbers=(((1,), (1,)), ((), ())),
-        preferred_element_type=jnp.float32,
-    )
-    width = rows_ref.shape[1]
-    row_inside = core * rows + lax.broadcasted_iota(jnp.int32, (half, 2 * rows), 0)
-    col_inside = lax.broadcasted_iota(jnp.int32, (half, 2 * rows), 1)
-
-    def multiply(h):
-        above = jnp.where(row_inside + h * half < col_inside, 1, 0)
-        for step, first, count in lists:
-            def make(i, carry, step=step, first=first):
-                col, _, _, _ = piece(x, chip, step, i, nx, half_tiles, half_x)
-                b_hi = chi[pl.ds(2 * col, 2)].reshape(2 * rows, width)
-                b_lo = clo[pl.ds(2 * col, 2)].reshape(2 * rows, width)
-                both = one(zsplit[step, h], b_hi)
-                full = both[:half] + (both[half:] + one(zsplit[step, h, :half], b_lo))
-                if step == 0:
-                    full = jnp.where(above * jnp.where(i == 0, 1, 0) == 1, 0.0, full)
-                pieces[h, first + i, 0] = full[:, :rows]
-                pieces[h, first + i, 1] = full[:, rows:]
-                return carry
-            lax.fori_loop(0, count, make, 0)
-
     def arrival(offset):
         return pl.ds(offset * capacity * 2, capacity * 2)
 
@@ -292,7 +311,7 @@
         if h == 1:
             take_other(half_x, 1)
             split_other(half_x, 1)
-        multiply(h)
+        multiply(h, "all" if h == 1 else "late")
         for offset in range(1, ny):
             for k in range(capacity):
                 outgoing[h, offset, 2 * k:2 * k + 2] = pieces[h, chosen[offset][k]]

time: 60.5 us -> 58 us (0.959)
  Pallas kernels: 56.8 us -> 54.3 us
    pallas_call x1, Pallas kernels: 56.8 us -> 54.3 us  [per_device(): pl.pallas_call(functools.partial(kernel, (nx, ny, half_tiles, half_x, cap...]
where the time goes in v3:
time: 58 us; the launch traced here: 56.8 us
  Pallas kernels  54.3 us (94%)
  local copies, waits for them, and re-layouts  2.51 us (4%)
    pallas_call x1, Pallas kernels, per_device(): pl.pallas_call(functools.partial(kernel, (nx, ny, half_tiles, half_x, cap...  54.3 us
    unnamed x1, local copies, waits for them, and re-layouts  2.51 us

profile of v3, /device:TPU:0, one launch (start us, length us, event | category | flops | bytes accessed | tf_op | source)
XLA Modules:
  0.0 56.8 jit_solution(13847068349267072085)
XLA Ops:
  0.0 54.3 %shard_map.37 = f32[5,256,256]{2,1,0:T(8,128)} custom-call(f32[128,1024]{1,0:T(8,128)} %rows_ref.1, s32[136]{0:T(256)} %owner_ref.1, s32[136]{0:T(256)} %slot_ref.1), custom_call_target="tpu_custom_call" | custom-call | tf_op jit(solution)/shard_map/pallas_call | solution.py:359
  54.3 2.5 %copy.5 = f32[5,256,256]{2,1,0:T(8,128)} copy(f32[5,256,256]{2,1,0:T(8,128)} %shard_map.37) | data formatting | bytes 2621440

commit v4 on v3

--- a/solution.py
+++ b/solution.py
@@ -242,10 +242,12 @@
         for step, first, count in lists:
             if mode == "early" and step >= soon:
                 continue
+            if (mode == "before" and step == half_x) or (mode == "after" and step < half_x):
+                continue
 
             def make(i, carry, step=step, first=first):
                 col, _, _, _ = piece(x, chip, step, i, nx, half_tiles, half_x)
-                if mode == "all" or step >= soon:
+                if mode in ("before", "after") or step >= soon:
                     one_piece(i, step, first, col)
                 else:
                     wanted = (col != farthest) if mode == "early" else (col == farthest)
@@ -309,9 +311,10 @@
 
     for h in (0, 1):
         if h == 1:
+            multiply(1, "before")
             take_other(half_x, 1)
             split_other(half_x, 1)
-        multiply(h, "all" if h == 1 else "late")
+        multiply(h, "after" if h == 1 else "late")
         for offset in range(1, ny):
             for k in range(capacity):
                 outgoing[h, offset, 2 * k:2 * k + 2] = pieces[h, chosen[offset][k]]

time: 58 us -> 58 us (level)
  no operation moved by 1% of the time
where the time goes in v4:
time: 58 us; the launch traced here: 56.8 us
  Pallas kernels  54.3 us (94%)
  local copies, waits for them, and re-layouts  2.51 us (4%)
    pallas_call x1, Pallas kernels, per_device(): pl.pallas_call(functools.partial(kernel, (nx, ny, half_tiles, half_x, cap...  54.3 us
    unnamed x1, local copies, waits for them, and re-layouts  2.51 us

profile of v4, /device:TPU:0, one launch (start us, length us, event | category | flops | bytes accessed | tf_op | source)
XLA Modules:
  0.0 56.8 jit_solution(340100315074201904)
XLA Ops:
  0.0 54.3 %shard_map.37 = f32[5,256,256]{2,1,0:T(8,128)} custom-call(f32[128,1024]{1,0:T(8,128)} %rows_ref.1, s32[136]{0:T(256)} %owner_ref.1, s32[136]{0:T(256)} %slot_ref.1), custom_call_target="tpu_custom_call" | custom-call | tf_op jit(solution)/shard_map/pallas_call | solution.py:362
  54.3 2.5 %copy.5 = f32[5,256,256]{2,1,0:T(8,128)} copy(f32[5,256,256]{2,1,0:T(8,128)} %shard_map.37) | data formatting | bytes 2621440
